TPU v7x, 32 devices: a whole 2x2x4 slice. The times are simulated.
32 devices in a mesh: site: 8 (over z, x), dom: 4 (over y, core).
Axes of the slice: x: 2, y: 2, z: 4, core: 2. Of those that a mesh axis runs over, the one named last changes fastest.
Arguments:
- top_partial: float32 [16, 61, 4, 8192], P(None, None, 'dom', 'site'), may hold values from 0.001 to 1
- bottom_partial: float32 [16, 61, 4, 8192], P(None, None, 'dom', 'site'), may hold values from 0.001 to 1
- left_vectors: float32 [256, 61, 61], P('dom'), may hold values from 0.05 to 1
- right_vectors: float32 [256, 61, 61], P('dom'), may hold values from 0.05 to 1
- decay_rates: float32 [256, 61], P('dom'), may hold values from 0.05 to 8
- state_weights: float32 [256, 61], P('dom'), may hold values from 0.002 to 0.05
- part_rates: float32 [256], P('dom'), may hold values from 0.3 to 3
- branch_lengths: float32 [1997], replicated, may hold values from 0.02 to 0.5
- pattern_weights: int32 [4, 8192], P('dom', 'site'), may hold values from 0 to 9
- block_partition: int32 [4, 64], P('dom', 'site'), may hold values from 0 to 255
- chosen_branches: int32 [16], replicated, may hold values from 0 to 1996, as said below
Outputs:
- site_loglik: float32 [16, 4, 8192], P(None, 'dom', 'site')
- part_derivs: float32 [2, 16, 256], P(None, None, 'dom')
- new_lengths: float32 [1997], replicated
Inputs may be any that keep to these rules, and one draw needn't show every extreme that they name: `chosen_branches`: distinct branch numbers.
All inputs are finite; a program needn't handle non-finite values.
Results may differ from a plain program's by a relative error of at most 0.0003.
Values sent between devices are 32-bit elements; how exact they have to be, the bound alone decides.
A program may use at most 64 MiB of HBM per device.

v0:
```python
import jax
import jax.numpy as jnp
from jax import lax
from jax.sharding import PartitionSpec as P

BLK = 128


def project(upper, lower, vec_left, vec_right, state_w):
    scaled = upper * jnp.transpose(state_w)[None, :, :, None]
    lefts = jnp.einsum("binl,nik->bknl", scaled, vec_left, precision=lax.Precision.HIGHEST)
    rights = jnp.einsum("nkj,bjnl->bknl", vec_right, lower, precision=lax.Precision.HIGHEST)
    return (lefts, rights)


def finish(lefts, rights, exponent, times, weight_f):
    joint = lefts * rights
    expo = jnp.transpose(exponent)[None, :, :, None]
    decayed = joint * jnp.exp(expo * times[:, None, None, None])
    like_zero = jnp.sum(decayed, axis=1)
    like_one = jnp.sum(decayed * expo, axis=1)
    like_two = jnp.sum(decayed * expo * expo, axis=1)
    first = like_one / like_zero
    second = like_two / like_zero - first * first
    loglik = weight_f[None] * jnp.log(like_zero)
    sums = jnp.stack(
        [jnp.sum(weight_f[None] * first, axis=-1), jnp.sum(weight_f[None] * second, axis=-1)]
    )
    return (loglik, sums)


def on_device(
    top_partial,
    bottom_partial,
    left_vectors,
    right_vectors,
    decay_rates,
    state_weights,
    part_rates,
    branch_lengths,
    pattern_weights,
    block_partition,
    chosen_branches,
):
    times = branch_lengths[chosen_branches]
    branches = top_partial.shape[0]
    states = top_partial.shape[1]
    sites_here = top_partial.shape[3]
    nblocks = sites_here // BLK
    upper = top_partial.reshape(branches, states, nblocks, BLK)
    lower = bottom_partial.reshape(branches, states, nblocks, BLK)
    blocks = block_partition[0]
    owned = left_vectors.shape[0]
    groups = lax.axis_size("dom")
    parts_all = owned * groups
    wanted = lax.all_gather(block_partition, "dom", axis=0, tiled=True)
    relative = wanted - lax.axis_index("dom") * owned
    inside = jnp.logical_and(relative >= 0, relative < owned).astype(jnp.float32)
    clipped = jnp.clip(relative, 0, owned - 1)
    send_left = left_vectors[clipped] * inside[:, :, None, None]
    send_right = right_vectors[clipped] * inside[:, :, None, None]
    send_decay = decay_rates[clipped] * inside[:, :, None]
    send_weight = state_weights[clipped] * inside[:, :, None]
    send_rate = part_rates[clipped] * inside
    received = (
        lax.all_to_all(send_left, "dom", split_axis=0, concat_axis=0, tiled=True),
        lax.all_to_all(send_right, "dom", split_axis=0, concat_axis=0, tiled=True),
        lax.all_to_all(send_decay, "dom", split_axis=0, concat_axis=0, tiled=True),
        lax.all_to_all(send_weight, "dom", split_axis=0, concat_axis=0, tiled=True),
        lax.all_to_all(send_rate, "dom", split_axis=0, concat_axis=0, tiled=True),
    )
    vec_left = jnp.sum(received[0], axis=0)
    vec_right = jnp.sum(received[1], axis=0)
    decay_b = jnp.sum(received[2], axis=0)
    weight_b = jnp.sum(received[3], axis=0)
    rate_b = jnp.sum(received[4], axis=0)
    exponent = -decay_b * rate_b[:, None]
    lefts, rights = project(upper, lower, vec_left, vec_right, weight_b)
    weight_f = pattern_weights[0].astype(jnp.float32).reshape(nblocks, BLK)
    loglik, sums = finish(lefts, rights, exponent, times, weight_f)
    onehot = (blocks[:, None] == jnp.arange(parts_all, dtype=jnp.int32)[None, :]).astype(
        jnp.float32
    )
    part_local = jnp.einsum("abn,np->abp", sums, onehot, precision=lax.Precision.HIGHEST)
    everything = lax.psum(part_local, ("site", "dom"))
    share = lax.dynamic_slice_in_dim(everything, lax.axis_index("dom") * owned, owned, 2)
    totals = jnp.sum(everything, axis=2)
    updated = times - totals[0] / totals[1]
    new_lengths = branch_lengths.at[chosen_branches].set(updated)
    return (loglik.reshape(branches, 1, sites_here), share, new_lengths)


def solution(mesh):
    return jax.shard_map(
        on_device,
        mesh=mesh,
        in_specs=(
            P(None, None, "dom", "site"),
            P(None, None, "dom", "site"),
            P("dom", None, None),
            P("dom", None, None),
            P("dom", None),
            P("dom", None),
            P("dom"),
            P(),
            P("dom", "site"),
            P("dom", "site"),
            P(),
        ),
        out_specs=(P(None, "dom", "site"), P(None, None, "dom"), P()),
        check_vma=False,
    )
```

profile of v0, /device:TPU:0, one launch (start us, length us, event | category | flops | bytes accessed | tf_op | source)
XLA Modules:
  0.0 121.8 jit_solution(4191838396032848199)
XLA Ops:
  0.6 0.8 copy.76
  1.5 6.2 %all-gather = s32[4,1,8]{2,1,0:T(1,128)S(1)} all-gather(s32[1,1,8]{2,1,0:T(1,128)} %bitcast.55), channel_id=1, replica_groups=mesh['site'=8,'dom'=4] {'dom'}, dimensions={0}, use_global_device_ids=true | all-gather | bytes 160 | tf_op jit(solution)/shard_map/all_gather | solution.py:56
  7.8 1.4 %gather_fusion.4 = f32[32]{0:T(128)S(1)} fusion(f32[64]{0:T(128)} %param.17, s32[1024]{0:T(1024)S(1)} %pad_clamp_fusion.1), kind=kCustom, calls=%fused_computation.4 | custom fusion | bytes 384 | tf_op jit(solution)/shard_map/gather | solution.py:64
  9.9 3.2 %all-to-all-start.4 = ((f32[4,1,8]{2,1,0:T(1,128)}), f32[4,1,8]{2,1,0:T(1,128)S(1)}, u32[]{:S(2)}, u32[]{:S(2)}) async-start(f32[4,1,8]{2,1,0:T(1,128)} %bitcast.14), calls=%async_computation.4 | async-start | bytes 4096 | tf_op jit(solution)/shard_map/all_to_all | solution.py:70
  13.1 1.3 %gather_fusion.3 = f32[32,61]{1,0:T(8,128)S(1)} fusion(f32[64,61]{1,0:T(8,128)} %param.15, s32[1024]{0:T(1024)S(1)} %pad_clamp_fusion.1), kind=kCustom, calls=%fused_computation.3 | custom fusion | bytes 15744 | tf_op jit(solution)/shard_map/gather | solution.py:62
  14.4 1.3 %gather_fusion.1 = f32[32,61]{1,0:T(8,128)S(1)} fusion(f32[64,61]{1,0:T(8,128)} %param.16, s32[1024]{0:T(1024)S(1)} %pad_clamp_fusion.1), kind=kCustom, calls=%fused_computation.1 | custom fusion | bytes 15744 | tf_op jit(solution)/shard_map/gather | solution.py:63
  16.8 3.2 %all-to-all-start.3 = ((f32[4,1,488]{2,1,0:T(1,128)}), f32[4,1,488]{2,1,0:T(1,128)S(1)}, u32[]{:S(2)}, u32[]{:S(2)}) async-start(f32[4,1,488]{2,1,0:T(1,128)} %reshape.156), calls=%async_computation.3 | async-start | bytes 16384 | tf_op jit(solution)/shard_map/all_to_all | solution.py:68
  20.7 2.7 %gather_fusion.2 = f32[32,61,61]{2,0,1:T(8,128)S(1)} fusion(f32[64,61,61]{2,0,1:T(8,128)S(1)} %copy-done, s32[1024]{0:T(1024)S(1)} %pad_clamp_fusion.1), kind=kCustom, calls=%fused_computation.2 | custom fusion | bytes 952704 | tf_op jit(solution)/shard_map/gather | solution.py:61
  23.5 5.3 %gather_fusion = f32[32,61,61]{2,0,1:T(8,128)} fusion(f32[64,61,61]{2,0,1:T(8,128)} %param.13, s32[1024]{0:T(1024)S(1)} %pad_clamp_fusion.1), kind=kCustom, calls=%fused_computation | custom fusion | bytes 952704 | tf_op jit(solution)/shard_map/gather | solution.py:60
  28.8 3.4 %all-to-all-start.1 = ((f32[4,1,488]{2,1,0:T(1,128)}), f32[4,1,488]{2,1,0:T(1,128)S(1)}, u32[]{:S(2)}, u32[]{:S(2)}) async-start(f32[4,1,488]{2,1,0:T(1,128)} %reshape.158), calls=%async_computation.1 | async-start | bytes 16384 | tf_op jit(solution)/shard_map/all_to_all | solution.py:69
  32.2 2.8 %copy_multiply_fusion.5 = (f32[4,8,61,61]{3,1,2,0:T(8,128)}, f32[4,8,61,61]{3,1,2,0:T(8,128)}) fusion(f32[4,8]{1,0:T(4,128)S(1)} %bitcast_convert_fusion, f32[32,61,61]{2,0,1:T(8,128)S(1)} %gather_fusion.2, f32[32,61,61]{2,0,1:T(8,128)} %gather_fusion), kind=kLoop, calls=%fused_computation.16 | loop fusion | flops 238144 | bytes 1905280 | tf_op jit(solution)/shard_map/mul | solution.py:60
  35.0 3.2 %reshape.160 = f32[4,1,29768]{2,1,0:T(1,128)} reshape(f32[4,61,8,61]{3,2,1,0:T(8,128)} %bitcast.46) | data formatting | bytes 952576
  38.2 3.5 %all-to-all-start = ((f32[4,1,29768]{2,1,0:T(1,128)}), f32[4,1,29768]{2,1,0:T(1,128)S(1)}, u32[]{:S(2)}, u32[]{:S(2)}) async-start(f32[4,1,29768]{2,1,0:T(1,128)} %reshape.160), calls=%async_computation | async-start | bytes 954368 | tf_op jit(solution)/shard_map/all_to_all | solution.py:66
  41.7 3.1 %reshape.154 = f32[4,1,29768]{2,1,0:T(1,128)} reshape(f32[4,61,8,61]{3,2,1,0:T(8,128)} %bitcast.45) | data formatting | bytes 952576
  48.3 1.7 %all-to-all-done = f32[4,1,29768]{2,1,0:T(1,128)S(1)} async-done(((f32[4,1,29768]{2,1,0:T(1,128)}), f32[4,1,29768]{2,1,0:T(1,128)S(1)}, u32[]{:S(2)}, u32[]{:S(2)}) %all-to-all-start) | async-done | bytes 476320 | tf_op jit(solution)/shard_map/all_to_all | solution.py:66
  49.9 4.3 %all-to-all-start.2 = ((f32[4,1,29768]{2,1,0:T(1,128)}), f32[4,1,29768]{2,1,0:T(1,128)}, u32[]{:S(2)}, u32[]{:S(2)}) async-start(f32[4,1,29768]{2,1,0:T(1,128)} %reshape.154), calls=%async_computation.2 | async-start | bytes 954368 | tf_op jit(solution)/shard_map/all_to_all | solution.py:67
  54.3 2.1 %reduce.4 = f32[4,29768]{1,0:T(4,128)S(1)} reduce(f32[4,1,29768]{2,1,0:T(1,128)S(1)} %all-to-all-done, f32[]{:T(128)} %broadcast.86), dimensions={1}, to_apply=%all_to_all.18.reduce_sub_computation | reduce | bytes 952580 | tf_op jit(solution)/shard_map/all_to_all | solution.py:66
  57.0 0.8 bitcast_reduce_fusion
  57.7 4.7 %all-to-all-done.2 = f32[4,1,29768]{2,1,0:T(1,128)} async-done(((f32[4,1,29768]{2,1,0:T(1,128)}), f32[4,1,29768]{2,1,0:T(1,128)}, u32[]{:S(2)}, u32[]{:S(2)}) %all-to-all-start.2) | async-done | bytes 476320 | tf_op jit(solution)/shard_map/all_to_all | solution.py:67
  62.4 2.9 %reduce.2 = f32[4,29768]{1,0:T(4,128)S(1)} reduce(f32[4,1,29768]{2,1,0:T(1,128)} %all-to-all-done.2, f32[]{:T(128)} %broadcast.86), dimensions={1}, to_apply=%all_to_all.20.reduce_sub_computation | reduce | bytes 952580 | tf_op jit(solution)/shard_map/all_to_all | solution.py:67
  66.0 6.8 %fusion = f32[8,61,16,128]{3,1,2,0:T(8,128)S(1)} fusion(f32[16,61,8,128]{3,2,1,0:T(8,128)} %bitcast.44, f32[8,61,61,1]{2,0,1,3:T(8,128)S(1)} %bitcast.47), kind=kOutput, calls=%fused_computation.8 | convolution fusion | flops 731578368 | bytes 8114464 | tf_op jit(solution)/shard_map/nkj,bjnl->bknl/dot_general | solution.py:12
  72.9 6.4 %multiply_reduce_fusion.1 = (f32[16,8,128]{2,0,1:T(8,128)S(1)}, f32[16,8,128]{2,0,1:T(8,128)S(1)}, f32[16,8,128]{2,0,1:T(8,128)S(1)}) fusion(f32[61,8]{0,1:T(8,128)S(1)} %copy-done.4, f32[16,61,8]{1,0,2:T(8,128)S(1)} %multiply_exponential_fusion, f32[8,61,16,128]{3,1,2,0:T(8,128)S(1)} %fusion, f32[16,61,8,128]{3,2,1,0:T(8,128)S(1)} %bitcast.57, ...), kind=kOutput, calls=%fused_computation.13 | convolution fusion | flops 739524608 | bytes 8346208 | tf_op jit(solution)/shard_map/binl,nik->bknl/dot_general | solution.py:11
  79.7 39.9 %psum.7 = f32[2,16,256]{2,1,0:T(8,128)S(1)} all-reduce(f32[2,16,256]{2,1,0:T(8,128)S(1)} %fusion.6), channel_id=1, replica_groups=mesh['site'=8,'dom'=4] {'site','dom'}, use_global_device_ids=true, to_apply=%region_10.11 | all-reduce | flops 8192 | bytes 65536 | tf_op jit(solution)/shard_map/psum | solution.py:85
  121.1 0.7 copy.45
  (68 shorter events, 9.1 us)
Async XLA Ops:
  0.6 20.1 %copy-start = (f32[64,61,61]{2,0,1:T(8,128)S(1)}, f32[64,61,61]{2,0,1:T(8,128)}, u32[]{:S(2)}) copy-start(f32[64,61,61]{2,0,1:T(8,128)} %param.14) | copy-start | bytes 2857732
  9.9 6.9 %all-to-all-start.4 = ((f32[4,1,8]{2,1,0:T(1,128)}), f32[4,1,8]{2,1,0:T(1,128)S(1)}, u32[]{:S(2)}, u32[]{:S(2)}) async-start(f32[4,1,8]{2,1,0:T(1,128)} %bitcast.14), calls=%async_computation.4 | async-start | bytes 4096 | tf_op jit(solution)/shard_map/all_to_all | solution.py:70
  16.8 12.0 %all-to-all-start.3 = ((f32[4,1,488]{2,1,0:T(1,128)}), f32[4,1,488]{2,1,0:T(1,128)S(1)}, u32[]{:S(2)}, u32[]{:S(2)}) async-start(f32[4,1,488]{2,1,0:T(1,128)} %reshape.156), calls=%async_computation.3 | async-start | bytes 16384 | tf_op jit(solution)/shard_map/all_to_all | solution.py:68
  28.8 12.9 %copy-start.13 = (s32[16]{0:T(128)S(1)}, s32[16]{0:T(128)}, u32[]{:S(2)}) copy-start(s32[16]{0:T(128)} %param.21) | copy-start | bytes 196
  28.8 12.9 %copy-start.7 = (s32[1,1024]{1,0:T(1,128)S(1)}, s32[1,1024]{1,0:T(1,128)}, u32[]{:S(2)}) copy-start(s32[1,1024]{1,0:T(1,128)} %param.19) | copy-start | bytes 12292
  28.8 9.4 %all-to-all-start.1 = ((f32[4,1,488]{2,1,0:T(1,128)}), f32[4,1,488]{2,1,0:T(1,128)S(1)}, u32[]{:S(2)}, u32[]{:S(2)}) async-start(f32[4,1,488]{2,1,0:T(1,128)} %reshape.158), calls=%async_computation.1 | async-start | bytes 16384 | tf_op jit(solution)/shard_map/all_to_all | solution.py:69
  38.2 11.8 %all-to-all-start = ((f32[4,1,29768]{2,1,0:T(1,128)}), f32[4,1,29768]{2,1,0:T(1,128)S(1)}, u32[]{:S(2)}, u32[]{:S(2)}) async-start(f32[4,1,29768]{2,1,0:T(1,128)} %reshape.160), calls=%async_computation | async-start | bytes 954368 | tf_op jit(solution)/shard_map/all_to_all | solution.py:66
  41.7 3.2 %copy-start.9 = (s32[16]{0:T(128)}, s32[16]{0:T(128)S(1)}, u32[]{:S(2)}) copy-start(s32[16]{0:T(128)S(1)} %compare_select_fusion.1) | copy-start | bytes 196
  45.5 8.7 %copy-start.5 = (f32[16]{0:T(128)}, f32[16]{0:T(128)S(1)}, u32[]{:S(2)}) copy-start(f32[16]{0:T(128)S(1)} %gather_fusion.5) | copy-start | bytes 196
  48.2 6.1 %copy-start.3 = (f32[61,8]{0,1:T(8,128)}, f32[61,8]{0,1:T(8,128)S(1)}, u32[]{:S(2)}) copy-start(f32[61,8]{0,1:T(8,128)S(1)} %multiply_bitcast_fusion) | copy-start | bytes 5860
  49.9 12.5 %all-to-all-start.2 = ((f32[4,1,29768]{2,1,0:T(1,128)}), f32[4,1,29768]{2,1,0:T(1,128)}, u32[]{:S(2)}, u32[]{:S(2)}) async-start(f32[4,1,29768]{2,1,0:T(1,128)} %reshape.154), calls=%async_computation.2 | async-start | bytes 954368 | tf_op jit(solution)/shard_map/all_to_all | solution.py:67
  66.0 6.9 %copy-start.2 = (f32[8,61,61]{2,0,1:T(8,128)S(1)}, f32[8,61,61]{2,0,1:T(8,128)}, u32[]{:S(2)}) copy-start(f32[8,61,61]{2,0,1:T(8,128)} %bitcast_reduce_fusion) | copy-start | bytes 357220
  66.0 6.9 %copy-start.4 = (f32[61,8]{0,1:T(8,128)S(1)}, f32[61,8]{0,1:T(8,128)}, u32[]{:S(2)}) copy-start(f32[61,8]{0,1:T(8,128)} %copy-done.3) | copy-start | bytes 5860
  66.0 6.9 %copy-start.8 = (f32[8,61]{1,0:T(8,128)S(1)}, f32[8,61]{1,0:T(8,128)}, u32[]{:S(2)}) copy-start(f32[8,61]{1,0:T(8,128)} %reduce_sum.100) | copy-start | bytes 5860
  66.0 6.9 %copy-start.12 = (f32[16,61,1,1024]{3,2,1,0:T(1,128)S(1)}, f32[16,61,1,1024]{3,2,1,0:T(1,128)}, u32[]{:S(2)}) copy-start(f32[16,61,1,1024]{3,2,1,0:T(1,128)} %param.11) | copy-start | bytes 11993092
  72.9 6.6 %copy-start.11 = (s32[1,8]{1,0:T(1,128)S(1)}, s32[1,8]{1,0:T(1,128)}, u32[]{:S(2)}) copy-start(s32[1,8]{1,0:T(1,128)} %param.20) | copy-start | bytes 100
  72.9 47.5 %copy-start.6 = (f32[16]{0:T(128)S(1)}, f32[16]{0:T(128)}, u32[]{:S(2)}) copy-start(f32[16]{0:T(128)} %copy-done.5) | copy-start | bytes 196
  72.9 47.5 %copy-start.10 = (s32[16]{0:T(128)S(1)}, s32[16]{0:T(128)}, u32[]{:S(2)}) copy-start(s32[16]{0:T(128)} %copy-done.9) | copy-start | bytes 196
  121.0 0.8 copy-start.1
where the time goes:
time: 123 us; the launch traced here: 122 us
  blocking collectives  46.1 us (37%)
  local copies, waits for them, and re-layouts  25.3 us (21%)
  starting transfers between devices  17.6 us (14%)
  matrix products  13.5 us (11%)
  other arithmetic  11.7 us (10%)
  waiting for transfers between devices  6.6 us (5%)
    psum x1, blocking collectives, on_device(): everything = lax.psum(part_local, ('site', 'dom'))  39.9 us
    unnamed x38, local copies, waits for them, and re-layouts  10.6 us
    dot_general x1, matrix products, project(): jnp.einsum('nkj,bjnl->bknl', vec_right, lower, precision=lax.Precision.HI...  6.82 us
    dot_general x1, matrix products, project(): jnp.einsum('binl,nik->bknl', scaled, vec_left, precision=lax.Precision.HI...  6.42 us
    all_gather x1, blocking collectives, on_device(): wanted = lax.all_gather(block_partition, 'dom', axis=0, tiled=True)  6.22 us
    gather x1, local copies, waits for them, and re-layouts, on_device(): send_left = left_vectors[clipped] * inside[:, :, None, None]  5.29 us
    all_to_all x1, waiting for transfers between devices, on_device(): lax.all_to_all(send_right, 'dom', split_axis=0, concat_axis=0, tiled=True)  4.67 us
    all_to_all x1, starting transfers between devices, on_device(): lax.all_to_all(send_right, 'dom', split_axis=0, concat_axis=0, tiled=True)  4.3 us
  transfers between devices with their start and end apart: 5, of which 3 were waited for; matrix products, arithmetic and copies ran while one was open for 23% of the time, Pallas kernels for 0%

commit v1 on v0

--- a/solution.py
+++ b/solution.py
@@ -42,6 +42,12 @@
     block_partition,
     chosen_branches,
 ):
+
+    def close_series(message, row_axis, named_axis):
+        current_arr = lax.psum(message, row_axis)
+        local_part = lax.psum(current_arr, named_axis)
+        return local_part
+
     times = branch_lengths[chosen_branches]
     branches = top_partial.shape[0]
     states = top_partial.shape[1]
@@ -82,7 +88,7 @@
         jnp.float32
     )
     part_local = jnp.einsum("abn,np->abp", sums, onehot, precision=lax.Precision.HIGHEST)
-    everything = lax.psum(part_local, ("site", "dom"))
+    everything = close_series(part_local, "dom", named_axis="site")
     share = lax.dynamic_slice_in_dim(everything, lax.axis_index("dom") * owned, owned, 2)
     totals = jnp.sum(everything, axis=2)
     updated = times - totals[0] / totals[1]

time: 123 us -> 131 us (1.065)
  blocking collectives: 46.1 us -> 54.1 us
    psum x1 -> x2, blocking collectives: 39.9 us -> 47.9 us  [the longest x1 37.6 us: close_series(): local_part = lax.psum(current_arr, named_axis)]
  transfers between devices with their start and end apart: 5 -> 5, of which waited for: 3 -> 3; matrix products, arithmetic and copies ran while one was open for 23% -> 22% of each run, Pallas kernels for 0% -> 0%
where the time goes in v1:
time: 131 us; the launch traced here: 130 us
  blocking collectives  54.1 us (41%)
  local copies, waits for them, and re-layouts  25.3 us (19%)
  starting transfers between devices  17.6 us (13%)
  matrix products  13.5 us (10%)
  other arithmetic  11.7 us (9%)
  waiting for transfers between devices  6.6 us (5%)
    psum x1, blocking collectives, close_series(): local_part = lax.psum(current_arr, named_axis)  37.6 us
    unnamed x38, local copies, waits for them, and re-layouts  10.6 us
    psum x1, blocking collectives, close_series(): current_arr = lax.psum(message, row_axis)  10.3 us
    dot_general x1, matrix products, project(): jnp.einsum('nkj,bjnl->bknl', vec_right, lower, precision=lax.Precision.HI...  6.82 us
    dot_general x1, matrix products, project(): jnp.einsum('binl,nik->bknl', scaled, vec_left, precision=lax.Precision.HI...  6.42 us
    all_gather x1, blocking collectives, on_device(): wanted = lax.all_gather(block_partition, 'dom', axis=0, tiled=True)  6.22 us
    gather x1, local copies, waits for them, and re-layouts, on_device(): send_left = left_vectors[clipped] * inside[:, :, None, None]  5.29 us
    all_to_all x1, waiting for transfers between devices, on_device(): lax.all_to_all(send_right, 'dom', split_axis=0, concat_axis=0, tiled=True)  4.67 us
  transfers between devices with their start and end apart: 5, of which 3 were waited for; matrix products, arithmetic and copies ran while one was open for 22% of the time, Pallas kernels for 0%

profile of v1, /device:TPU:0, one launch (start us, length us, event | category | flops | bytes accessed | tf_op | source)
XLA Modules:
  0.0 129.8 jit_solution(9390500443762465183)
XLA Ops:
  0.6 0.8 copy.76
  1.5 6.2 %all-gather = s32[4,1,8]{2,1,0:T(1,128)S(1)} all-gather(s32[1,1,8]{2,1,0:T(1,128)} %bitcast.55), channel_id=1, replica_groups=mesh['site'=8,'dom'=4] {'dom'}, dimensions={0}, use_global_device_ids=true | all-gather | bytes 160 | tf_op jit(solution)/shard_map/all_gather | solution.py:62
  7.8 1.4 %gather_fusion.4 = f32[32]{0:T(128)S(1)} fusion(f32[64]{0:T(128)} %param.17, s32[1024]{0:T(1024)S(1)} %pad_clamp_fusion.1), kind=kCustom, calls=%fused_computation.4 | custom fusion | bytes 384 | tf_op jit(solution)/shard_map/gather | solution.py:70
  9.9 3.2 %all-to-all-start.4 = ((f32[4,1,8]{2,1,0:T(1,128)}), f32[4,1,8]{2,1,0:T(1,128)S(1)}, u32[]{:S(2)}, u32[]{:S(2)}) async-start(f32[4,1,8]{2,1,0:T(1,128)} %bitcast.14), calls=%async_computation.4 | async-start | bytes 4096 | tf_op jit(solution)/shard_map/all_to_all | solution.py:76
  13.1 1.3 %gather_fusion.3 = f32[32,61]{1,0:T(8,128)S(1)} fusion(f32[64,61]{1,0:T(8,128)} %param.15, s32[1024]{0:T(1024)S(1)} %pad_clamp_fusion.1), kind=kCustom, calls=%fused_computation.3 | custom fusion | bytes 15744 | tf_op jit(solution)/shard_map/gather | solution.py:68
  14.4 1.3 %gather_fusion.1 = f32[32,61]{1,0:T(8,128)S(1)} fusion(f32[64,61]{1,0:T(8,128)} %param.16, s32[1024]{0:T(1024)S(1)} %pad_clamp_fusion.1), kind=kCustom, calls=%fused_computation.1 | custom fusion | bytes 15744 | tf_op jit(solution)/shard_map/gather | solution.py:69
  16.8 3.2 %all-to-all-start.3 = ((f32[4,1,488]{2,1,0:T(1,128)}), f32[4,1,488]{2,1,0:T(1,128)S(1)}, u32[]{:S(2)}, u32[]{:S(2)}) async-start(f32[4,1,488]{2,1,0:T(1,128)} %reshape.156), calls=%async_computation.3 | async-start | bytes 16384 | tf_op jit(solution)/shard_map/all_to_all | solution.py:74
  20.7 2.7 %gather_fusion.2 = f32[32,61,61]{2,0,1:T(8,128)S(1)} fusion(f32[64,61,61]{2,0,1:T(8,128)S(1)} %copy-done, s32[1024]{0:T(1024)S(1)} %pad_clamp_fusion.1), kind=kCustom, calls=%fused_computation.2 | custom fusion | bytes 952704 | tf_op jit(solution)/shard_map/gather | solution.py:67
  23.5 5.3 %gather_fusion = f32[32,61,61]{2,0,1:T(8,128)} fusion(f32[64,61,61]{2,0,1:T(8,128)} %param.13, s32[1024]{0:T(1024)S(1)} %pad_clamp_fusion.1), kind=kCustom, calls=%fused_computation | custom fusion | bytes 952704 | tf_op jit(solution)/shard_map/gather | solution.py:66
  28.8 3.4 %all-to-all-start.1 = ((f32[4,1,488]{2,1,0:T(1,128)}), f32[4,1,488]{2,1,0:T(1,128)S(1)}, u32[]{:S(2)}, u32[]{:S(2)}) async-start(f32[4,1,488]{2,1,0:T(1,128)} %reshape.158), calls=%async_computation.1 | async-start | bytes 16384 | tf_op jit(solution)/shard_map/all_to_all | solution.py:75
  32.2 2.8 %copy_multiply_fusion.5 = (f32[4,8,61,61]{3,1,2,0:T(8,128)}, f32[4,8,61,61]{3,1,2,0:T(8,128)}) fusion(f32[4,8]{1,0:T(4,128)S(1)} %bitcast_convert_fusion, f32[32,61,61]{2,0,1:T(8,128)S(1)} %gather_fusion.2, f32[32,61,61]{2,0,1:T(8,128)} %gather_fusion), kind=kLoop, calls=%fused_computation.16 | loop fusion | flops 238144 | bytes 1905280 | tf_op jit(solution)/shard_map/mul | solution.py:66
  35.0 3.2 %reshape.160 = f32[4,1,29768]{2,1,0:T(1,128)} reshape(f32[4,61,8,61]{3,2,1,0:T(8,128)} %bitcast.46) | data formatting | bytes 952576
  38.2 3.5 %all-to-all-start = ((f32[4,1,29768]{2,1,0:T(1,128)}), f32[4,1,29768]{2,1,0:T(1,128)S(1)}, u32[]{:S(2)}, u32[]{:S(2)}) async-start(f32[4,1,29768]{2,1,0:T(1,128)} %reshape.160), calls=%async_computation | async-start | bytes 954368 | tf_op jit(solution)/shard_map/all_to_all | solution.py:72
  41.7 3.1 %reshape.154 = f32[4,1,29768]{2,1,0:T(1,128)} reshape(f32[4,61,8,61]{3,2,1,0:T(8,128)} %bitcast.45) | data formatting | bytes 952576
  48.3 1.7 %all-to-all-done = f32[4,1,29768]{2,1,0:T(1,128)S(1)} async-done(((f32[4,1,29768]{2,1,0:T(1,128)}), f32[4,1,29768]{2,1,0:T(1,128)S(1)}, u32[]{:S(2)}, u32[]{:S(2)}) %all-to-all-start) | async-done | bytes 476320 | tf_op jit(solution)/shard_map/all_to_all | solution.py:72
  49.9 4.3 %all-to-all-start.2 = ((f32[4,1,29768]{2,1,0:T(1,128)}), f32[4,1,29768]{2,1,0:T(1,128)}, u32[]{:S(2)}, u32[]{:S(2)}) async-start(f32[4,1,29768]{2,1,0:T(1,128)} %reshape.154), calls=%async_computation.2 | async-start | bytes 954368 | tf_op jit(solution)/shard_map/all_to_all | solution.py:73
  54.3 2.1 %reduce.4 = f32[4,29768]{1,0:T(4,128)S(1)} reduce(f32[4,1,29768]{2,1,0:T(1,128)S(1)} %all-to-all-done, f32[]{:T(128)} %broadcast.86), dimensions={1}, to_apply=%all_to_all.18.reduce_sub_computation | reduce | bytes 952580 | tf_op jit(solution)/shard_map/all_to_all | solution.py:72
  57.0 0.8 bitcast_reduce_fusion
  57.7 4.7 %all-to-all-done.2 = f32[4,1,29768]{2,1,0:T(1,128)} async-done(((f32[4,1,29768]{2,1,0:T(1,128)}), f32[4,1,29768]{2,1,0:T(1,128)}, u32[]{:S(2)}, u32[]{:S(2)}) %all-to-all-start.2) | async-done | bytes 476320 | tf_op jit(solution)/shard_map/all_to_all | solution.py:73
  62.4 2.9 %reduce.2 = f32[4,29768]{1,0:T(4,128)S(1)} reduce(f32[4,1,29768]{2,1,0:T(1,128)} %all-to-all-done.2, f32[]{:T(128)} %broadcast.86), dimensions={1}, to_apply=%all_to_all.20.reduce_sub_computation | reduce | bytes 952580 | tf_op jit(solution)/shard_map/all_to_all | solution.py:73
  66.0 6.8 %fusion = f32[8,61,16,128]{3,1,2,0:T(8,128)S(1)} fusion(f32[16,61,8,128]{3,2,1,0:T(8,128)} %bitcast.44, f32[8,61,61,1]{2,0,1,3:T(8,128)S(1)} %bitcast.47), kind=kOutput, calls=%fused_computation.8 | convolution fusion | flops 731578368 | bytes 8114464 | tf_op jit(solution)/shard_map/nkj,bjnl->bknl/dot_general | solution.py:12
  72.9 6.4 %multiply_reduce_fusion.1 = (f32[16,8,128]{2,0,1:T(8,128)S(1)}, f32[16,8,128]{2,0,1:T(8,128)S(1)}, f32[16,8,128]{2,0,1:T(8,128)S(1)}) fusion(f32[61,8]{0,1:T(8,128)S(1)} %copy-done.4, f32[16,61,8]{1,0,2:T(8,128)S(1)} %multiply_exponential_fusion, f32[8,61,16,128]{3,1,2,0:T(8,128)S(1)} %fusion, f32[16,61,8,128]{3,2,1,0:T(8,128)S(1)} %bitcast.57, ...), kind=kOutput, calls=%fused_computation.13 | convolution fusion | flops 739524608 | bytes 8346208 | tf_op jit(solution)/shard_map/binl,nik->bknl/dot_general | solution.py:11
  79.7 10.3 %psum.14 = f32[2,16,256]{2,1,0:T(8,128)S(1)} all-reduce(f32[2,16,256]{2,1,0:T(8,128)S(1)} %fusion.6), channel_id=1, replica_groups=mesh['site'=8,'dom'=4] {'dom'}, use_global_device_ids=true, to_apply=%region_10.11 | all-reduce | flops 8192 | bytes 65536 | tf_op jit(solution)/shard_map/psum | solution.py:47
  90.0 37.6 %psum.15 = f32[2,16,256]{2,1,0:T(8,128)S(1)} all-reduce(f32[2,16,256]{2,1,0:T(8,128)S(1)} %psum.14), channel_id=1, replica_groups=mesh['site'=8,'dom'=4] {'site'}, use_global_device_ids=true, to_apply=%region_11.12 | all-reduce | flops 8192 | bytes 65536 | tf_op jit(solution)/shard_map/psum | solution.py:48
  (69 shorter events, 9.8 us)
Async XLA Ops:
  0.6 20.1 %copy-start = (f32[64,61,61]{2,0,1:T(8,128)S(1)}, f32[64,61,61]{2,0,1:T(8,128)}, u32[]{:S(2)}) copy-start(f32[64,61,61]{2,0,1:T(8,128)} %param.14) | copy-start | bytes 2857732
  9.9 6.9 %all-to-all-start.4 = ((f32[4,1,8]{2,1,0:T(1,128)}), f32[4,1,8]{2,1,0:T(1,128)S(1)}, u32[]{:S(2)}, u32[]{:S(2)}) async-start(f32[4,1,8]{2,1,0:T(1,128)} %bitcast.14), calls=%async_computation.4 | async-start | bytes 4096 | tf_op jit(solution)/shard_map/all_to_all | solution.py:76
  16.8 12.0 %all-to-all-start.3 = ((f32[4,1,488]{2,1,0:T(1,128)}), f32[4,1,488]{2,1,0:T(1,128)S(1)}, u32[]{:S(2)}, u32[]{:S(2)}) async-start(f32[4,1,488]{2,1,0:T(1,128)} %reshape.156), calls=%async_computation.3 | async-start | bytes 16384 | tf_op jit(solution)/shard_map/all_to_all | solution.py:74
  28.8 12.9 %copy-start.13 = (s32[16]{0:T(128)S(1)}, s32[16]{0:T(128)}, u32[]{:S(2)}) copy-start(s32[16]{0:T(128)} %param.21) | copy-start | bytes 196
  28.8 12.9 %copy-start.7 = (s32[1,1024]{1,0:T(1,128)S(1)}, s32[1,1024]{1,0:T(1,128)}, u32[]{:S(2)}) copy-start(s32[1,1024]{1,0:T(1,128)} %param.19) | copy-start | bytes 12292
  28.8 9.4 %all-to-all-start.1 = ((f32[4,1,488]{2,1,0:T(1,128)}), f32[4,1,488]{2,1,0:T(1,128)S(1)}, u32[]{:S(2)}, u32[]{:S(2)}) async-start(f32[4,1,488]{2,1,0:T(1,128)} %reshape.158), calls=%async_computation.1 | async-start | bytes 16384 | tf_op jit(solution)/shard_map/all_to_all | solution.py:75
  38.2 11.8 %all-to-all-start = ((f32[4,1,29768]{2,1,0:T(1,128)}), f32[4,1,29768]{2,1,0:T(1,128)S(1)}, u32[]{:S(2)}, u32[]{:S(2)}) async-start(f32[4,1,29768]{2,1,0:T(1,128)} %reshape.160), calls=%async_computation | async-start | bytes 954368 | tf_op jit(solution)/shard_map/all_to_all | solution.py:72
  41.7 3.2 %copy-start.9 = (s32[16]{0:T(128)}, s32[16]{0:T(128)S(1)}, u32[]{:S(2)}) copy-start(s32[16]{0:T(128)S(1)} %compare_select_fusion.1) | copy-start | bytes 196
  45.5 8.7 %copy-start.5 = (f32[16]{0:T(128)}, f32[16]{0:T(128)S(1)}, u32[]{:S(2)}) copy-start(f32[16]{0:T(128)S(1)} %gather_fusion.5) | copy-start | bytes 196
  48.2 6.1 %copy-start.3 = (f32[61,8]{0,1:T(8,128)}, f32[61,8]{0,1:T(8,128)S(1)}, u32[]{:S(2)}) copy-start(f32[61,8]{0,1:T(8,128)S(1)} %multiply_bitcast_fusion) | copy-start | bytes 5860
  49.9 12.5 %all-to-all-start.2 = ((f32[4,1,29768]{2,1,0:T(1,128)}), f32[4,1,29768]{2,1,0:T(1,128)}, u32[]{:S(2)}, u32[]{:S(2)}) async-start(f32[4,1,29768]{2,1,0:T(1,128)} %reshape.154), calls=%async_computation.2 | async-start | bytes 954368 | tf_op jit(solution)/shard_map/all_to_all | solution.py:73
  66.0 6.9 %copy-start.2 = (f32[8,61,61]{2,0,1:T(8,128)S(1)}, f32[8,61,61]{2,0,1:T(8,128)}, u32[]{:S(2)}) copy-start(f32[8,61,61]{2,0,1:T(8,128)} %bitcast_reduce_fusion) | copy-start | bytes 357220
  66.0 6.9 %copy-start.4 = (f32[61,8]{0,1:T(8,128)S(1)}, f32[61,8]{0,1:T(8,128)}, u32[]{:S(2)}) copy-start(f32[61,8]{0,1:T(8,128)} %copy-done.3) | copy-start | bytes 5860
  66.0 6.9 %copy-start.8 = (f32[8,61]{1,0:T(8,128)S(1)}, f32[8,61]{1,0:T(8,128)}, u32[]{:S(2)}) copy-start(f32[8,61]{1,0:T(8,128)} %reduce_sum.100) | copy-start | bytes 5860
  66.0 6.9 %copy-start.12 = (f32[16,61,1,1024]{3,2,1,0:T(1,128)S(1)}, f32[16,61,1,1024]{3,2,1,0:T(1,128)}, u32[]{:S(2)}) copy-start(f32[16,61,1,1024]{3,2,1,0:T(1,128)} %param.11) | copy-start | bytes 11993092
  72.9 6.6 %copy-start.11 = (s32[1,8]{1,0:T(1,128)S(1)}, s32[1,8]{1,0:T(1,128)}, u32[]{:S(2)}) copy-start(s32[1,8]{1,0:T(1,128)} %param.20) | copy-start | bytes 100
  72.9 55.5 %copy-start.6 = (f32[16]{0:T(128)S(1)}, f32[16]{0:T(128)}, u32[]{:S(2)}) copy-start(f32[16]{0:T(128)} %copy-done.5) | copy-start | bytes 196
  72.9 55.5 %copy-start.10 = (s32[16]{0:T(128)S(1)}, s32[16]{0:T(128)}, u32[]{:S(2)}) copy-start(s32[16]{0:T(128)} %copy-done.9) | copy-start | bytes 196
  129.1 0.8 copy-start.1
